TPU v7x, 32 devices: a whole 2x2x4 slice. The times are simulated.
32 devices in a mesh: leaf: 16 (over z, y, x), player: 2 (over core).
Axes of the slice: x: 2, y: 2, z: 4, core: 2. Of those that a mesh axis runs over, the one named last changes fastest.
Arguments:
- chance_reach: float32 [2, 512, 1326], P('player', 'leaf'), may hold values from 0.02 to 1
- regrets_start: float32 [2, 512, 1326], P('player', 'leaf'), may hold values from -6 to 6
- pot: float32 [512], P('leaf'), may hold values from 1 to 8
- parent: int32 [2, 512], P('player'), may hold values from 0 to 255, never falling along the last dimension, each value on 1 to 6 neighbouring positions
- hand_cards: int32 [1326, 2], replicated, may hold values from 0 to 51, as said below
- board_cards: int32 [64, 5], P('leaf'), may hold values from 0 to 51, as said below
- hand_rank: int32 [64, 1326], P('leaf'), may hold values from 0 to 1999
Outputs:
- regrets: float32 [2, 512, 1326], P('player', 'leaf')
- values: float32 [2, 512, 1326], P('player', 'leaf')
Inputs may be any that keep to these rules, and one draw needn't show every extreme that they name: `parent`: along each row the node ids never fall; each node owns 1 to 6 consecutive leaves, one exactly 6; every id up to 255 occurs. `hand_cards`: distinct pairs of two different cards, the smaller card first. `board_cards`: five different cards on each board.
All inputs are finite; a program needn't handle non-finite values.
Results may differ from a plain program's by a relative error of at most 0.0003.
Values sent between devices are 32-bit elements; how exact they have to be, the bound alone decides.
A program may use at most 128 MiB of HBM per device.

v0:
```python
import functools

import jax
import jax.numpy as jnp
from jax import lax
from jax.experimental import pallas as pl
from jax.experimental.pallas import tpu as pltpu
from jax.sharding import PartitionSpec as P

ITERS = 2
MOST = 6
DELTA = 0.05
EPSILON = 1e-06
DECK_SIZE = 52
LANES = 128
WIDE = 256
SPLIT = 5
MESH = pl.DeviceIdType.MESH
F32 = jnp.float32
BF16 = jnp.bfloat16


def round_up(value, unit):
    return (value + unit - 1) // unit * unit


def column_of(row, count):
    down = lax.broadcasted_iota(jnp.int32, (count, count), 0)
    across = lax.broadcasted_iota(jnp.int32, (count, count), 1)
    return jnp.sum(jnp.where(down == across, row, 0.0), axis=1, keepdims=True)


def row_of(column, count):
    down = lax.broadcasted_iota(jnp.int32, (count, count), 0)
    across = lax.broadcasted_iota(jnp.int32, (count, count), 1)
    return jnp.sum(jnp.where(down == across, column, 0.0), axis=0, keepdims=True)


def kernel(
    n, boards, rows, hands, leaf_count,
    chance_far, regrets_far, pot_far, parent_far, cards_far, board_cards_far, rank_far,
    out_regrets, out_values,
    chance, regrets, pot, parent, cards, board_cards, rank, load,
    payoff, left, right, free, cards_wide, rank_wide, pots, same, split,
    held, policy, reach, opposed, values, square_out, square_in,
    held_send, held_recv, value_send, value_recv, reach_send, reach_recv, square_send, square_recv,
):
    me = lax.axis_index("leaf")
    player = lax.axis_index("player")
    before, after = lax.rem(me + n - 1, n), lax.rem(me + 1, n)
    width = payoff.shape[1]
    depth = left.shape[0]
    chunks = boards + 2
    total = chunks * rows

    loads = [
        pltpu.make_async_copy(far, near, load.at[i])
        for i, (far, near) in enumerate((
            (cards_far, cards), (board_cards_far, board_cards), (rank_far, rank), (regrets_far, regrets),
            (pot_far, pot), (parent_far, parent), (chance_far, chance)))]
    for copy in loads:
        copy.start()

    zeros = jnp.zeros((rows, hands), F32)
    for edge in (0, chunks - 1):
        held[edge] = zeros
        for it in range(ITERS):
            values[it, edge] = zeros

    barrier = pltpu.get_barrier_semaphore()

    def greet(k, carry):
        pl.semaphore_signal(barrier, inc=1, device_id={"leaf": lax.rem(me + k, n)}, device_id_type=MESH)
        return carry

    pl.semaphore_signal(barrier, inc=1, device_id={"player": 1 - player}, device_id_type=MESH)
    lax.fori_loop(1, n, greet, 0)

    for copy in loads[:3]:
        copy.wait()

    cards_wide[...] = jnp.full(cards_wide.shape, -1, jnp.int32)
    cards_wide[:, :hands] = cards[...]
    rank_wide[...] = jnp.zeros(rank_wide.shape, jnp.int32)
    rank_wide[:boards, :hands] = rank[...]
    card = lax.broadcasted_iota(jnp.int32, (depth, width), 0)
    lane = lax.broadcasted_iota(jnp.int32, (depth, width), 1)
    holding = ((card == cards_wide[0:1, :]) | (card == cards_wide[1:2, :])).astype(F32)
    valid = ((card == depth - 1) & (lane < hands)).astype(F32)
    ranked = rank_wide[...]
    code = ((128 + (ranked & 127)) << (ranked >> 7)).astype(F32)
    left[...] = holding + valid
    left[DECK_SIZE : DECK_SIZE + boards, :] = code[:boards]
    right[:, :width] = (valid - holding).astype(BF16)
    pick = lax.broadcasted_iota(jnp.int32, (depth, boards * LANES), 0) - DECK_SIZE
    spot = lax.broadcasted_iota(jnp.int32, (depth, boards * LANES), 1)
    right[:, width:] = ((spot >= pick * LANES) & (spot < pick * LANES + LANES)).astype(BF16)
    deck = lax.broadcasted_iota(jnp.int32, (boards, depth), 1)
    on_board = jnp.zeros((boards, depth), jnp.bool_)
    for k in range(board_cards.shape[1]):
        on_board = on_board | (deck == board_cards[:, k : k + 1])
    touched = jnp.dot(on_board.astype(BF16), holding.astype(BF16), preferred_element_type=F32)
    free[...] = (touched < 0.5).astype(F32)

    def build(i, carry):
        start = pl.multiple_of(i * LANES, LANES)
        down = left[:, pl.ds(start, LANES)].T.astype(BF16)
        lows = jnp.dot(down, right[:, width:], preferred_element_type=F32).astype(BF16)
        for first in range(0, width, WIDE):
            last = min(first + WIDE, width)
            apart = jnp.dot(down, right[:, first:last], preferred_element_type=F32)
            apart = jnp.maximum(apart.astype(BF16), 0.0)
            for at in range(first, last, LANES):
                highs = [
                    jnp.broadcast_to(left[DECK_SIZE + b : DECK_SIZE + b + 1, at : at + LANES], (16, LANES)).astype(BF16)
                    for b in range(boards)]
                for r in range(0, LANES, 16):
                    bound = apart[r : r + 16, at - first : at - first + LANES]
                    floor = -bound
                    for b in range(boards):
                        gap = highs[b] - lows[r : r + 16, b * LANES : (b + 1) * LANES]
                        payoff[b, pl.ds(start + r, 16), at : at + LANES] = jnp.minimum(
                            jnp.maximum(gap, floor), bound)
        return carry

    blocks = width // LANES
    lax.fori_loop(0, SPLIT, build, 0)

    for copy in loads[3:]:
        copy.wait()
    pl.semaphore_wait(barrier, n)

    def to_before(source, target, send, recv):
        return pltpu.make_async_remote_copy(
            src_ref=source, dst_ref=target, send_sem=send, recv_sem=recv,
            device_id={"leaf": before}, device_id_type=MESH)

    def to_after(source, target, send, recv):
        return pltpu.make_async_remote_copy(
            src_ref=source, dst_ref=target, send_sem=send, recv_sem=recv,
            device_id={"leaf": after}, device_id_type=MESH)

    reach_of = min(MOST - 1, rows)
    held_down = to_before(
        regrets.at[0, pl.ds(0, reach_of)], held.at[chunks - 1, pl.ds(0, reach_of)], held_send.at[0], held_recv.at[0])
    held_up = to_after(
        regrets.at[0, pl.ds(boards * rows - reach_of, reach_of)], held.at[0, pl.ds(rows - reach_of, reach_of)], held_send.at[1], held_recv.at[1])
    value_down = [
        to_before(
            values.at[it, 1, pl.ds(0, reach_of)], values.at[it, chunks - 1, pl.ds(0, reach_of)], value_send.at[it, 0], value_recv.at[it, 0])
        for it in range(ITERS)]
    value_up = [
        to_after(
            values.at[it, boards, pl.ds(rows - reach_of, reach_of)], values.at[it, 0, pl.ds(rows - reach_of, reach_of)],
            value_send.at[it, 1], value_recv.at[it, 1])
        for it in range(ITERS)]

    @pl.when(me > 0)
    def _():
        held_down.start()

    @pl.when(me < n - 1)
    def _():
        held_up.start()

    twice = lax.broadcasted_iota(jnp.int32, (2 * total, leaf_count), 0)
    leaf = me * (boards * rows) - rows + jnp.where(twice >= total, twice - total, twice)
    here = lax.broadcasted_iota(jnp.int32, (2 * total, leaf_count), 1)
    ids = jnp.sum(jnp.where(leaf == here, parent[...].astype(F32) + 1.0, 0.0), axis=1, keepdims=True)
    same[...] = (ids[:total] == row_of(ids, 2 * total)).astype(BF16)
    pots[...] = jnp.broadcast_to(
        column_of(pot[...], boards * rows) * (1.0 / hands), (boards * rows, LANES)).reshape(boards, rows, LANES)
    split[...] = jnp.zeros(split.shape, BF16)
    for b in range(boards):
        held[b + 1] = regrets[0, pl.ds(b * rows, rows)]

    lax.fori_loop(SPLIT, blocks, build, 0)

    def node_totals(array):
        coarse = array.astype(BF16)
        fine = (array - coarse.astype(F32)).astype(BF16)
        return jnp.dot(same[...], jnp.concatenate([coarse, fine], axis=0), preferred_element_type=F32)

    @pl.when(me > 0)
    def _():
        held_up.wait_recv()

    @pl.when(me < n - 1)
    def _():
        held_down.wait_recv()

    standing = held[...].reshape(total, hands)
    for it in range(ITERS):
        positive = jnp.maximum(standing, 0.0) + DELTA
        policy[it] = positive / node_totals(positive)
        own_policy = policy[it, rows : rows + boards * rows]
        reach[it] = (chance[0] * own_policy).reshape(boards, rows, hands)

        def exchange(b, it=it):
            return pltpu.make_async_remote_copy(
                src_ref=reach.at[it, b], dst_ref=opposed.at[it, b],
                send_sem=reach_send.at[it, b], recv_sem=reach_recv.at[it, b],
                device_id={"player": 1 - player}, device_id_type=MESH)

        for t in range(boards):
            exchange(t * (boards - 1) % boards).start()

        def showdown(t, carry, it=it, exchange=exchange):
            b = lax.rem(t * (boards - 1), boards)
            exchange(b).wait_recv()
            open_hands = free[pl.ds(b, 1), :]
            facing = opposed[it, b] * open_hands[:, :hands]
            coarse = facing.astype(BF16).astype(F32)
            split[:, :hands] = jnp.concatenate([coarse, facing - coarse], axis=0).astype(BF16)
            summed = jnp.dot(split[...], payoff[b], preferred_element_type=F32)
            summed = (summed[:rows] + summed[rows:]) * open_hands * pots[b][:, :1]
            values[it, b + 1] = summed[:, :hands]

            @pl.when((t == 0) & (me > 0))
            def _():
                value_down[it].start()

            @pl.when((t == 1) & (me < n - 1))
            def _():
                value_up[it].start()

            return carry

        lax.fori_loop(0, boards, showdown, 0)

        @pl.when(me > 0)
        def _(it=it):
            value_up[it].wait_recv()

        @pl.when(me < n - 1)
        def _(it=it):
            value_down[it].wait_recv()

        gained = values[it].reshape(total, hands)
        instant = gained - node_totals(policy[it] * gained)
        own = instant[rows : rows + boards * rows]
        squares = jnp.sum(jnp.sum(own * own, axis=0, keepdims=True), axis=1, keepdims=True)
        square_out[it] = jnp.broadcast_to(squares, (1, LANES))

        def tell(k, carry, it=it):
            pltpu.make_async_remote_copy(
                src_ref=square_out.at[it], dst_ref=square_in.at[it, k - 1],
                send_sem=square_send.at[it], recv_sem=square_recv.at[it],
                device_id={"leaf": lax.rem(me + k, n)}, device_id_type=MESH).start()
            return carry

        lax.fori_loop(1, n, tell, 0)
        if it == ITERS - 1:
            out_values[0] = gained[rows : rows + boards * rows]
        everyone = square_in.at[it]
        pltpu.make_async_copy(everyone, everyone, square_recv.at[it]).wait()
        squares = square_out[it] + jnp.sum(square_in[it], axis=0)
        inverse = 1.0 / jnp.sqrt(squares[:, :1] / (leaf_count * hands) + EPSILON)
        if it < ITERS - 1:
            standing = standing + instant * inverse
        else:
            out_regrets[0] = standing[rows : rows + boards * rows] + own * inverse

    @pl.when(me > 0)
    def _():
        held_down.wait_send()
        for it in range(ITERS):
            value_down[it].wait_send()

    @pl.when(me < n - 1)
    def _():
        held_up.wait_send()
        for it in range(ITERS):
            value_up[it].wait_send()

    for it in range(ITERS):
        everyone = square_in.at[it]
        pltpu.make_async_copy(everyone, everyone, square_send.at[it]).wait()
        for b in range(boards):
            pltpu.make_async_copy(reach.at[it, b], reach.at[it, b], reach_send.at[it, b]).wait()


def solution(mesh):
    n = mesh.shape["leaf"]

    def local(chance_reach, regrets_start, pot, parent, hand_cards, board_cards, hand_rank):
        leaf_rows, hands = chance_reach.shape[1:]
        boards = hand_rank.shape[0]
        rows = leaf_rows // boards
        leaf_count = parent.shape[1]
        width = round_up(hands, LANES)
        depth = round_up(DECK_SIZE + boards + 1, 16)
        chunks = boards + 2
        vmem = pl.BlockSpec(memory_space=pltpu.VMEM)
        shape = pltpu.VMEM(chance_reach.shape, F32)
        dma = pltpu.SemaphoreType.DMA
        arrays = (chance_reach, regrets_start, pot[None], parent, hand_cards.T, board_cards, hand_rank)
        return pl.pallas_call(
            functools.partial(kernel, n, boards, rows, hands, leaf_count),
            out_shape=(shape, shape),
            in_specs=[pl.BlockSpec(memory_space=pl.ANY)] * len(arrays),
            out_specs=(vmem, vmem),
            scratch_shapes=[
                *(pltpu.VMEM(array.shape, array.dtype) for array in arrays),
                pltpu.SemaphoreType.DMA((len(arrays),)),
                pltpu.VMEM((boards, width, width), BF16),
                pltpu.VMEM((depth, width), F32),
                pltpu.VMEM((depth, width + boards * LANES), BF16),
                pltpu.VMEM((boards, width), F32),
                pltpu.VMEM((2, width), jnp.int32),
                pltpu.VMEM((round_up(boards, 8), width), jnp.int32),
                pltpu.VMEM((boards, rows, LANES), F32),
                pltpu.VMEM((chunks * rows, 2 * chunks * rows), BF16),
                pltpu.VMEM((2 * rows, width), BF16),
                pltpu.VMEM((chunks, rows, hands), F32),
                pltpu.VMEM((ITERS, chunks * rows, hands), F32),
                pltpu.VMEM((ITERS, boards, rows, hands), F32),
                pltpu.VMEM((ITERS, boards, rows, hands), F32),
                pltpu.VMEM((ITERS, chunks, rows, hands), F32),
                pltpu.VMEM((ITERS, 1, LANES), F32),
                pltpu.VMEM((ITERS, n - 1, 1, LANES), F32),
                dma((2,)), dma((2,)),
                dma((ITERS, 2)), dma((ITERS, 2)),
                dma((ITERS, boards)), dma((ITERS, boards)),
                dma((ITERS,)), dma((ITERS,)),
            ],
            compiler_params=pltpu.CompilerParams(collective_id=0, has_side_effects=True),
            name="regret",
        )(*arrays)

    in_specs = (
        P("player", "leaf", None),
        P("player", "leaf", None),
        P("leaf"),
        P("player", None),
        P(),
        P("leaf", None),
        P("leaf", None),
    )
    out_specs = (P("player", "leaf", None), P("player", "leaf", None))
    return jax.shard_map(local, mesh=mesh, in_specs=in_specs, out_specs=out_specs, check_vma=False)
```

profile of v0, /device:TPU:0, one launch (start us, length us, event | category | flops | bytes accessed | tf_op | source)
XLA Modules:
  0.0 32.8 jit_solution(10644122367460631349)
XLA Ops:
  0.6 30.8 %regret.1 = (f32[1,32,1326]{2,1,0:T(8,128)S(1)}, f32[1,32,1326]{2,1,0:T(8,128)S(1)}) custom-call(f32[1,32,1326]{2,1,0:T(8,128)} %chance_far.1, f32[1,32,1326]{2,1,0:T(8,128)} %regrets_far.1, f32[1,32]{1,0:T(1,128)} %bitcast.3, s32[1,512]{1,0:T(1,128)} %parent_far.1, s32[2,1326]{1,0:T(2,128)} %bitcast.2, s32[4,5]{1,0:T(4,128)} %board_cards_far.1, ...), custom_call_target="tpu_custom_call" | custom-call | tf_op jit(solution)/shard_map/regret/pallas_call | solution.py:298
  31.4 0.7 %copy.11 = f32[1,32,1326]{2,1,0:T(8,128)} copy(f32[1,32,1326]{2,1,0:T(8,128)S(1)} %get-tuple-element.2) | data formatting | bytes 339456
  32.1 0.7 %copy.12 = f32[1,32,1326]{2,1,0:T(8,128)} copy(f32[1,32,1326]{2,1,0:T(8,128)S(1)} %get-tuple-element.3) | data formatting | bytes 339456
where the time goes:
time: 33 us; the launch traced here: 32.8 us
  Pallas kernels  30.8 us (93%)
  local copies, waits for them, and re-layouts  1.35 us (4%)
  between operations  0.64 us (2%)
    pallas_call x1, Pallas kernels, local(): pl.pallas_call(functools.partial(kernel, n, boards, rows, hands, leaf_cou...  30.8 us
    unnamed x2, local copies, waits for them, and re-layouts  1.35 us

commit v1 on v0

v1 whole, which is shorter than its diff:
```python
import functools

import jax
import jax.numpy as jnp
from jax import lax
from jax.experimental import pallas as pl
from jax.experimental.pallas import tpu as pltpu
from jax.sharding import PartitionSpec as P

ITERS = 2
MOST = 6
DELTA = 0.05
EPSILON = 1e-06
DECK_SIZE = 52
LANES = 128
WIDE = 256
SPLIT = 4
PARTS = 2
MESH = pl.DeviceIdType.MESH
F32 = jnp.float32
BF16 = jnp.bfloat16

(GET_HALF, GET_BEFORE, GET_AFTER, GET_BEYOND, GET_CHANCE, GET_CHANCE_AFTER, GET_PARENT, GET_INFO,
 GET_LOW, GET_HIGH, GET_HIGHER, GET_VALUES, GET_EDGE_LOW, GET_EDGE_HIGH, GET_POLICY, GET_REGRETS, GETS) = (
    0, 1, 3, 5, 7, 8, 10, 11, 12, 13, 14, 15, 16, 17, 18, 19, 20)
(PUT_HALF, PUT_AFTER, PUT_BEFORE, PUT_BEYOND, PUT_CHANCE, PUT_CHANCE_BEFORE, PUT_PARENT, PUT_INFO,
 PUT_HIGH, PUT_LOW, PUT_LOWER, PUT_VALUES, PUT_EDGE, PUT_POLICY, PUT_REGRETS, PUTS) = (
    0, 1, 2, 3, 4, 5, 6, 7, 8, 9, 10, 11, 12, 14, 15, 16)


def round_up(value, unit):
    return (value + unit - 1) // unit * unit


def row_of(column, count):
    down = lax.broadcasted_iota(jnp.int32, (count, count), 0)
    across = lax.broadcasted_iota(jnp.int32, (count, count), 1)
    return jnp.sum(jnp.where(down == across, column, 0.0), axis=0, keepdims=True)


def same_of(ids):
    twice = jnp.concatenate([ids, ids], axis=0)
    return (ids == row_of(twice, twice.shape[0])).astype(BF16)


def node_totals(same, array):
    coarse = array.astype(BF16)
    fine = (array - coarse.astype(F32)).astype(BF16)
    return jnp.dot(same, jnp.concatenate([coarse, fine], axis=0), preferred_element_type=F32)


def settle(view, semaphore):
    pltpu.make_async_copy(view, view, semaphore).wait()


def body(
    n, boards, rows, hands, leaf_count,
    chance_far, regrets_far, pot_far, parent_far, cards_far, board_cards_far, rank_far,
    out_regrets, out_values,
    chance, regrets, pot, parents, cards, board_cards, rank, load,
    left, free, cards_wide, rank_wide, info, info_in, pots, weight,
    held, chances, policy, values, landed, standing_one, square_out, square_in,
    last_policy, last_regrets, last_values,
    all_in, put, get, square_send, square_recv,
    payoff, apart, turned, lows, right, same, same_own, same_last, split,
):
    me = lax.axis_index("leaf")
    player = lax.axis_index("player")
    other = 1 - player
    spot = 2 * me + player
    hub = 2 * n - 1
    width = free.shape[1]
    depth = left.shape[0]
    half = boards // 2
    near = half + 1
    local = boards * rows
    own = half * rows
    span = near * rows
    total = own + 3 * rows
    edge = min(MOST - 1, rows)
    rest = 2 * edge - rows
    last = ITERS - 1
    partner = {"player": other}

    def push(source, target, device, sent, received):
        pltpu.make_async_remote_copy(
            src_ref=source, dst_ref=target, send_sem=put.at[sent], recv_sem=get.at[received],
            device_id=device, device_id_type=MESH).start()

    def device_at(at):
        return {"leaf": at // 2, "player": at % 2}

    loads = [
        pltpu.make_async_copy(far, near_ref, load.at[i])
        for i, (far, near_ref) in enumerate((
            (cards_far, cards), (board_cards_far, board_cards), (rank_far, rank), (pot_far, pot), (regrets_far, regrets),
            (parent_far, parents.at[player]), (chance_far, chance)))]
    for copy in loads:
        copy.start()

    for p in range(2):
        held[p, :rows] = jnp.zeros((rows, hands), F32)
        held[p, rows + own :] = jnp.zeros((2 * rows, hands), F32)
        chances[p, own:] = jnp.zeros((rows, hands), F32)
        values[0, p, :rows] = jnp.zeros((rows, hands), F32)
        landed[p] = jnp.zeros((2 * rows, hands), F32)
    last_values[:rows] = jnp.zeros((rows, hands), F32)
    last_values[rows + local :] = jnp.zeros((rows, hands), F32)

    barrier = pltpu.get_barrier_semaphore()

    def greet(device):
        pl.semaphore_signal(barrier, inc=1, device_id=device, device_id_type=MESH)

    greet(partner)

    @pl.when((player == 0) & (me > 0))
    def _():
        for p in range(2):
            greet({"leaf": me - 1, "player": p})

    @pl.when((player == 1) & (me < n - 1))
    def _():
        for p in range(2):
            greet({"leaf": me + 1, "player": p})

    @pl.when(spot < hub - 2)
    def _():
        greet({"leaf": n - 1, "player": 1})

    for copy in loads[:4]:
        copy.wait()

    cards_wide[...] = jnp.full(cards_wide.shape, -1, jnp.int32)
    cards_wide[:, :hands] = cards[...]
    rank_wide[...] = jnp.zeros(rank_wide.shape, jnp.int32)
    rank_wide[:boards, :hands] = rank[...]
    card = lax.broadcasted_iota(jnp.int32, (depth, width), 0)
    lane = lax.broadcasted_iota(jnp.int32, (depth, width), 1)
    holding = ((card == cards_wide[0:1, :]) | (card == cards_wide[1:2, :])).astype(F32)
    valid = ((card == depth - 1) & (lane < hands)).astype(F32)
    ranked = rank_wide[...]
    code = ((128 + (ranked & 127)) << (ranked >> 7)).astype(F32)
    deck = lax.broadcasted_iota(jnp.int32, (boards, depth), 1)
    on_board = jnp.zeros((boards, depth), jnp.bool_)
    for k in range(board_cards.shape[1]):
        on_board = on_board | (deck == board_cards[:, k : k + 1])
    touched = jnp.dot(on_board.astype(BF16), holding.astype(BF16), preferred_element_type=F32)
    untouched = (touched < 0.5).astype(F32)
    first = player == 0
    left[...] = holding + valid
    left[DECK_SIZE : DECK_SIZE + half, :] = jnp.where(first, code[:half], code[half:boards])
    left[DECK_SIZE + half : DECK_SIZE + near, :] = code[half : half + 1]
    free[:half] = jnp.where(first, untouched[:half], untouched[half:])
    free[half:near] = untouched[half : half + 1]
    right[:, :width] = (valid - holding).astype(BF16)
    pick = lax.broadcasted_iota(jnp.int32, (depth, near * LANES), 0) - DECK_SIZE
    at_lane = lax.broadcasted_iota(jnp.int32, (depth, near * LANES), 1)
    right[:, width:] = ((at_lane >= pick * LANES) & (at_lane < pick * LANES + LANES)).astype(BF16)
    info[...] = jnp.zeros(info.shape, F32)
    info[:, :width] = code[:1]
    info[:, width : 2 * width] = untouched[:1]
    info[:, 2 * width : 2 * width + local] = pot[...]
    down = lax.broadcasted_iota(jnp.int32, (span, local), 0)
    across = lax.broadcasted_iota(jnp.int32, (span, local), 1)
    pots[...] = jnp.broadcast_to(
        jnp.sum(jnp.where(across == down + player * own, pot[...] * (1.0 / hands), 0.0), axis=1, keepdims=True),
        (span, LANES))
    split[...] = jnp.zeros(split.shape, BF16)

    turned[...] = left[...].T.astype(BF16)

    blocks = width // LANES
    length = width // PARTS

    def separate(first, last):
        for c in range(first, last, 2):
            found = jnp.dot(
                turned[...], right[:, c * LANES : min(c + 2, blocks) * LANES], preferred_element_type=F32).astype(BF16)
            for k in range(min(2, blocks - c)):
                apart[c + k] = found[:, k * LANES : (k + 1) * LANES].reshape(PARTS, length, LANES)

    def lower(begin, count):
        found = jnp.dot(
            turned[...], right[:, width + begin * LANES : width + (begin + count) * LANES],
            preferred_element_type=F32).astype(BF16)
        for b in range(count):
            lows[b] = found[:, b * LANES : (b + 1) * LANES].reshape(PARTS, length, LANES)

    def build(begin, count):
        def column(c, carry):
            at = pl.multiple_of(c * LANES, LANES)
            highs = [
                jnp.broadcast_to(
                    left[DECK_SIZE + begin + b : DECK_SIZE + begin + b + 1, pl.ds(at, LANES)], (16, LANES)).astype(BF16)
                for b in range(count)]

            def part(k, carry):
                for r in range(0, length, 16):
                    bound = apart[c, k, r : r + 16]
                    floor = -bound
                    for b in range(count):
                        gap = highs[b] - lows[b, k, r : r + 16]
                        payoff[begin + b, c, k, r : r + 16] = jnp.minimum(jnp.maximum(gap, floor), bound)
                return carry

            return lax.fori_loop(0, PARTS, part, carry)

        return column

    separate(0, blocks)
    lower(0, half)
    lax.fori_loop(0, SPLIT, build(0, half), 0)

    for copy in loads[4:]:
        copy.wait()

    @pl.when(spot < hub)
    def _():
        pl.semaphore_wait(barrier, 1 + (me > 0).astype(jnp.int32) + (me < n - 1).astype(jnp.int32))

    @pl.when(spot == hub)
    def _():
        pl.semaphore_wait(barrier, 2 * n - 1)

        def welcome(k, carry):
            pl.semaphore_signal(
                all_in, inc=1, device_id=device_at(lax.rem(spot + k, 2 * n)), device_id_type=MESH)
            return carry

        lax.fori_loop(1, 2 * n, welcome, 0)

    @pl.when(me > 0)
    def _():
        to = {"leaf": me - 1, "player": 1}

        @pl.when(player == 1)
        def _():
            push(info, info_in, to, PUT_INFO, GET_INFO)

        push(regrets.at[0, pl.ds(0, rows)], held.at[player, pl.ds(rows + own, rows)], to, PUT_BEFORE, GET_AFTER + player)
        push(
            regrets.at[0, pl.ds(rows, rest)], held.at[player, pl.ds(2 * rows + own, rest)], to, PUT_BEYOND,
            GET_BEYOND + player)
        push(chance.at[0, pl.ds(0, edge)], chances.at[player, pl.ds(own, edge)], to, PUT_CHANCE_BEFORE, GET_CHANCE_AFTER + player)

    @pl.when(me < n - 1)
    def _():
        push(
            regrets.at[0, pl.ds(local - edge, edge)], held.at[player, pl.ds(rows - edge, edge)],
            {"leaf": me + 1, "player": 0}, PUT_AFTER, GET_BEFORE + player)

    push(parents.at[player], parents.at[player], partner, PUT_PARENT, GET_PARENT)

    @pl.when(player == 0)
    def _():
        push(regrets.at[0, pl.ds(own - rows, own + rows)], held.at[0, pl.ds(0, own + rows)], partner, PUT_HALF, GET_HALF)
        push(chance.at[0, pl.ds(own, own)], chances.at[0, pl.ds(0, own)], partner, PUT_CHANCE, GET_CHANCE)
        held[0, rows:] = regrets[0, : own + 2 * rows]
        chances[0] = chance[0, :span]

    @pl.when(player == 1)
    def _():
        push(regrets.at[0, pl.ds(0, own + 2 * rows)], held.at[1, pl.ds(rows, own + 2 * rows)], partner, PUT_HALF, GET_HALF)
        push(chance.at[0, pl.ds(0, span)], chances.at[1], partner, PUT_CHANCE, GET_CHANCE)
        held[1, : own + rows] = regrets[0, own - rows :]
        chances[1, :own] = chance[0, own:]

    lax.fori_loop(SPLIT, blocks, build(0, half), 0)

    settle(parents.at[other], get.at[GET_PARENT])

    def ids_of(p, begin, count):
        leaf = begin + lax.broadcasted_iota(jnp.int32, (count, leaf_count), 0)
        here = lax.broadcasted_iota(jnp.int32, (count, leaf_count), 1)
        return jnp.sum(jnp.where(leaf == here, parents[p].astype(F32) + 1.0, 0.0), axis=1, keepdims=True)

    ids = []
    weights = []
    order = lax.broadcasted_iota(jnp.int32, (span, 1), 0)
    for p in range(2):
        found = ids_of(p, spot * own - rows, total)
        found = jnp.where(found > 0.0, found + p * (leaf_count + 1.0), 0.0)
        inside = found[rows : rows + span]
        counted = (inside > 0.0) & (inside != found[rows - 1 : rows])
        counted = counted & ((order < own) | (inside == found[rows + own - 1 : rows + own]))
        ids.append(found)
        weights.append(counted.astype(F32))
    same[...] = same_of(jnp.concatenate(ids, axis=0))
    same_own[...] = same_of(jnp.concatenate([found[rows : rows + span] for found in ids], axis=0))
    same_last[...] = same_of(ids_of(player, me * local - rows, local + 2 * rows))
    weight[...] = jnp.broadcast_to(jnp.concatenate(weights, axis=0), (2 * span, LANES))

    @pl.when((player == 1) & (me < n - 1))
    def _():
        settle(info_in, get.at[GET_INFO])
        left[DECK_SIZE + half : DECK_SIZE + near, :] = info_in[:, :width]
        free[half:near] = info_in[:, width : 2 * width]
        pots[own:] = jnp.broadcast_to(
            jnp.sum(
                jnp.where(across[:rows] == down[:rows], info_in[:, 2 * width : 2 * width + local] * (1.0 / hands), 0.0),
                axis=1, keepdims=True),
            (rows, LANES))

    turned[...] = left[...].T.astype(BF16)
    lower(half, 1)
    lax.fori_loop(0, blocks, build(half, 1), 0)

    @pl.when((player == 0) & (me > 0))
    def _():
        for p in range(2):
            settle(held.at[p, pl.ds(rows - edge, edge)], get.at[GET_BEFORE + p])

    @pl.when((player == 1) & (me < n - 1))
    def _():
        for p in range(2):
            settle(held.at[p, pl.ds(rows + own, rows)], get.at[GET_AFTER + p])
            settle(held.at[p, pl.ds(2 * rows + own, rest)], get.at[GET_BEYOND + p])
            settle(chances.at[p, pl.ds(own, edge)], get.at[GET_CHANCE_AFTER + p])

    @pl.when(player == 0)
    def _():
        settle(held.at[1, pl.ds(rows, own + 2 * rows)], get.at[GET_HALF])
        settle(chances.at[1], get.at[GET_CHANCE])

    @pl.when(player == 1)
    def _():
        settle(held.at[0, pl.ds(0, own + rows)], get.at[GET_HALF])
        settle(chances.at[0, pl.ds(0, own)], get.at[GET_CHANCE])

    standing = held[...].reshape(2 * total, hands)
    for it in range(ITERS):
        positive = jnp.maximum(standing, 0.0) + DELTA
        policy[it] = (positive / node_totals(same[...], positive)).reshape(2, total, hands)
        if it == last:
            standing_one[...] = standing.reshape(2, total, hands)
            push(
                policy.at[it, other, pl.ds(pl.multiple_of(player * rows, rows), span)],
                last_policy.at[pl.ds(pl.multiple_of(player * span, rows), span)], partner, PUT_POLICY, GET_POLICY)
            push(
                standing_one.at[other, pl.ds(rows, own)], last_regrets.at[pl.ds(pl.multiple_of(player * own, rows), own)],
                partner, PUT_REGRETS, GET_REGRETS)

        for b in range(near):
            seen = slice(b * rows, (b + 1) * rows)
            kept = slice((b + 1) * rows, (b + 2) * rows)
            open_hands = free[b : b + 1, :]
            facing = jnp.concatenate([chances[p, seen] * policy[it, p, kept] for p in range(2)], axis=0)
            facing = facing * open_hands[:, :hands]
            coarse = facing.astype(BF16).astype(F32)
            split[b, :, :hands] = jnp.concatenate([coarse, facing - coarse], axis=0).astype(BF16)
            summed = jnp.concatenate([
                jnp.dot(
                    split[b],
                    jnp.concatenate([payoff[b, k].reshape(width, LANES) for k in range(c, min(c + 2, blocks))], axis=1),
                    preferred_element_type=F32)
                for c in range(0, blocks, 2)], axis=1)
            stake = jnp.concatenate([pots[seen, :1]] * 2, axis=0)
            summed = (summed[: 2 * rows] + summed[2 * rows :])[:, :hands] + facing
            summed = summed * open_hands[:, :hands] * stake
            values[it, 1, kept] = summed[:rows]
            values[it, 0, kept] = summed[rows:]
            if b == half - 1 and it < last:
                @pl.when(spot < hub)
                def _(it=it):
                    push(
                        values.at[it, :, pl.ds(rows + own - edge, edge)], values.at[it, :, pl.ds(rows - edge, edge)],
                        device_at(spot + 1), PUT_HIGH, GET_LOW)

                @pl.when(spot > 0)
                def _(it=it):
                    push(
                        values.at[it, :, pl.ds(rows + edge, rows - edge)], landed.at[:, pl.ds(edge, rows - edge)],
                        device_at(spot - 1), PUT_LOW, GET_HIGH)
                    push(
                        values.at[it, :, pl.ds(2 * rows, rest)], landed.at[:, pl.ds(rows, rest)],
                        device_at(spot - 1), PUT_LOWER, GET_HIGHER)
            if b == half - 1 and it == last:
                push(
                    values.at[it, other, pl.ds(rows, own)],
                    last_values.at[pl.ds(pl.multiple_of(rows + player * own, rows), own)], partner, PUT_VALUES, GET_VALUES)

                @pl.when((player == 1) & (me < n - 1))
                def _(it=it):
                    for p in range(2):
                        push(
                            values.at[it, p, pl.ds(rows + own - edge, edge)], last_values.at[pl.ds(rows - edge, edge)],
                            {"leaf": me + 1, "player": p}, PUT_EDGE + p, GET_EDGE_LOW)

                @pl.when((player == 0) & (me > 0))
                def _(it=it):
                    for p in range(2):
                        push(
                            values.at[it, p, pl.ds(rows, edge)], last_values.at[pl.ds(rows + local, edge)],
                            {"leaf": me - 1, "player": p}, PUT_EDGE + p, GET_EDGE_HIGH)

        gained = jnp.concatenate([values[it, p, rows : rows + span] for p in range(2)], axis=0)
        played = jnp.concatenate([policy[it, p, rows : rows + span] for p in range(2)], axis=0)
        instant = (gained - node_totals(same_own[...], played * gained)) * weight[:, :1]
        squares = jnp.sum((instant * instant).reshape(2, span, hands), axis=1)
        square_out[it] = jnp.broadcast_to(jnp.sum(squares, axis=1, keepdims=True), (2, LANES))

        if it == 0:
            @pl.when(spot < hub)
            def _():
                pl.semaphore_wait(all_in, 1)

        def tell(k, carry, it=it):
            pltpu.make_async_remote_copy(
                src_ref=square_out.at[it], dst_ref=square_in.at[it, k - 1],
                send_sem=square_send.at[it], recv_sem=square_recv.at[it],
                device_id=device_at(lax.rem(spot + k, 2 * n)), device_id_type=MESH).start()
            return carry

        lax.fori_loop(1, 2 * n, tell, 0)

        if it < last:
            @pl.when(spot > 0)
            def _(it=it):
                settle(values.at[it, :, pl.ds(rows - edge, edge)], get.at[GET_LOW])

            @pl.when(spot < hub)
            def _():
                settle(landed.at[:, pl.ds(edge, rows - edge)], get.at[GET_HIGH])
                settle(landed.at[:, pl.ds(rows, rest)], get.at[GET_HIGHER])

            inner = lax.broadcasted_iota(jnp.int32, (rows, hands), 0) < edge
            gained = jnp.concatenate([
                part for p in range(2) for part in (
                    values[it, p, : rows + own], jnp.where(inner, values[it, p, rows + own : rows + span], landed[p, :rows]),
                    landed[p, rows:])], axis=0)
            instant = gained - node_totals(same[...], policy[it].reshape(2 * total, hands) * gained)
        else:
            mine = pl.ds(pl.multiple_of(player * span, rows), span)
            last_policy[mine] = policy[it, player, pl.ds(pl.multiple_of(player * rows, rows), span)]
            last_regrets[pl.ds(pl.multiple_of(player * own, rows), own)] = standing_one[player, pl.ds(rows, own)]
            last_values[pl.ds(pl.multiple_of(rows + player * own, rows), own)] = values[it, player, pl.ds(rows, own)]
            settle(last_policy.at[pl.ds(pl.multiple_of(other * span, rows), span)], get.at[GET_POLICY])
            settle(last_regrets.at[pl.ds(pl.multiple_of(other * own, rows), own)], get.at[GET_REGRETS])
            settle(last_values.at[pl.ds(pl.multiple_of(rows + other * own, rows), own)], get.at[GET_VALUES])

            @pl.when(me > 0)
            def _():
                settle(last_values.at[pl.ds(rows - edge, edge)], get.at[GET_EDGE_LOW])

            @pl.when(me < n - 1)
            def _():
                settle(last_values.at[pl.ds(rows + local, edge)], get.at[GET_EDGE_HIGH])

            gained = last_values[...]
            instant = (gained - node_totals(same_last[...], last_policy[...] * gained))[rows : rows + local]
            out_values[0] = gained[rows : rows + local]

        everyone = square_in.at[it]
        settle(everyone, square_recv.at[it])

        squares = square_out[it] + jnp.sum(square_in[it], axis=0)
        inverse = 1.0 / jnp.sqrt(squares / (leaf_count * hands) + EPSILON)
        if it < last:
            turn = lax.broadcasted_iota(jnp.int32, (2 * total, 1), 0) < total
            standing = standing + instant * jnp.where(turn, inverse[0:1, :1], inverse[1:2, :1])
        else:
            out_regrets[0] = last_regrets[...] + instant * jnp.where(player == 0, inverse[0:1, :1], inverse[1:2, :1])

    def sent(view, slot):
        settle(view, put.at[slot])

    @pl.when(me > 0)
    def _():
        @pl.when(player == 1)
        def _():
            sent(info, PUT_INFO)

        sent(regrets.at[0, pl.ds(0, rows)], PUT_BEFORE)
        sent(regrets.at[0, pl.ds(rows, rest)], PUT_BEYOND)
        sent(chance.at[0, pl.ds(0, edge)], PUT_CHANCE_BEFORE)

    @pl.when(me < n - 1)
    def _():
        sent(regrets.at[0, pl.ds(local - edge, edge)], PUT_AFTER)

    sent(parents.at[player], PUT_PARENT)

    @pl.when(player == 0)
    def _():
        sent(regrets.at[0, pl.ds(own - rows, own + rows)], PUT_HALF)
        sent(chance.at[0, pl.ds(own, own)], PUT_CHANCE)

    @pl.when(player == 1)
    def _():
        sent(regrets.at[0, pl.ds(0, own + 2 * rows)], PUT_HALF)
        sent(chance.at[0, pl.ds(0, span)], PUT_CHANCE)

    for it in range(last):
        @pl.when(spot < hub)
        def _(it=it):
            sent(values.at[it, :, pl.ds(rows + own - edge, edge)], PUT_HIGH)

        @pl.when(spot > 0)
        def _(it=it):
            sent(values.at[it, :, pl.ds(rows + edge, rows - edge)], PUT_LOW)
            sent(values.at[it, :, pl.ds(2 * rows, rest)], PUT_LOWER)

    sent(policy.at[last, other, pl.ds(pl.multiple_of(player * rows, rows), span)], PUT_POLICY)
    sent(standing_one.at[other, pl.ds(rows, own)], PUT_REGRETS)
    sent(values.at[last, other, pl.ds(rows, own)], PUT_VALUES)

    @pl.when((player == 1) & (me < n - 1))
    def _():
        for p in range(2):
            sent(values.at[last, p, pl.ds(rows + own - edge, edge)], PUT_EDGE + p)

    @pl.when((player == 0) & (me > 0))
    def _():
        for p in range(2):
            sent(values.at[last, p, pl.ds(rows, edge)], PUT_EDGE + p)

    for it in range(ITERS):
        everyone = square_in.at[it]
        settle(everyone, square_send.at[it])


def kernel(n, boards, rows, hands, leaf_count, *refs):
    near = boards // 2 + 1
    span = near * rows
    total = span + 2 * rows
    edged = (boards + 2) * rows
    width = round_up(hands, LANES)
    depth = round_up(DECK_SIZE + near + 1, 16)
    pl.run_scoped(
        functools.partial(body, n, boards, rows, hands, leaf_count, *refs),
        pltpu.VMEM((near, width // LANES, PARTS, width // PARTS, LANES), BF16),
        pltpu.VMEM((width // LANES, PARTS, width // PARTS, LANES), BF16),
        pltpu.VMEM((width, depth), BF16),
        pltpu.VMEM((near, PARTS, width // PARTS, LANES), BF16),
        pltpu.VMEM((depth, width + near * LANES), BF16),
        pltpu.VMEM((2 * total, 4 * total), BF16),
        pltpu.VMEM((2 * span, 4 * span), BF16),
        pltpu.VMEM((edged, 2 * edged), BF16),
        pltpu.VMEM((near, 4 * rows, width), BF16),
    )


def solution(mesh):
    n = mesh.shape["leaf"]

    def local(chance_reach, regrets_start, pot, parent, hand_cards, board_cards, hand_rank):
        leaf_rows, hands = chance_reach.shape[1:]
        boards = hand_rank.shape[0]
        rows = leaf_rows // boards
        leaf_count = parent.shape[1]
        width = round_up(hands, LANES)
        half = boards // 2
        near = half + 1
        depth = round_up(DECK_SIZE + near + 1, 16)
        span = near * rows
        total = (half + 3) * rows
        edged = leaf_rows + 2 * rows
        vmem = pl.BlockSpec(memory_space=pltpu.VMEM)
        shape = pltpu.VMEM(chance_reach.shape, F32)
        dma = pltpu.SemaphoreType.DMA
        arrays = (chance_reach, regrets_start, pot[None], parent, hand_cards.T, board_cards, hand_rank)
        return pl.pallas_call(
            functools.partial(kernel, n, boards, rows, hands, leaf_count),
            out_shape=(shape, shape),
            in_specs=[pl.BlockSpec(memory_space=pl.ANY)] * len(arrays),
            out_specs=(vmem, vmem),
            scratch_shapes=[
                pltpu.VMEM(chance_reach.shape, F32),
                pltpu.VMEM(regrets_start.shape, F32),
                pltpu.VMEM((1, leaf_rows), F32),
                pltpu.VMEM((2, 1, leaf_count), jnp.int32),
                pltpu.VMEM((2, hands), jnp.int32),
                pltpu.VMEM(board_cards.shape, jnp.int32),
                pltpu.VMEM(hand_rank.shape, jnp.int32),
                dma((len(arrays),)),
                pltpu.VMEM((depth, width), F32),
                pltpu.VMEM((near, width), F32),
                pltpu.VMEM((2, width), jnp.int32),
                pltpu.VMEM((round_up(boards, 8), width), jnp.int32),
                pltpu.VMEM((1, 2 * width + LANES), F32),
                pltpu.VMEM((1, 2 * width + LANES), F32),
                pltpu.VMEM((span, LANES), F32),
                pltpu.VMEM((2 * span, LANES), F32),
                pltpu.VMEM((2, total, hands), F32),
                pltpu.VMEM((2, span, hands), F32),
                pltpu.VMEM((ITERS, 2, total, hands), F32),
                pltpu.VMEM((ITERS, 2, total, hands), F32),
                pltpu.VMEM((2, 2 * rows, hands), F32),
                pltpu.VMEM((2, total, hands), F32),
                pltpu.VMEM((ITERS, 2, LANES), F32),
                pltpu.VMEM((ITERS, 2 * n - 1, 2, LANES), F32),
                pltpu.VMEM((edged, hands), F32),
                pltpu.VMEM((leaf_rows, hands), F32),
                pltpu.VMEM((edged, hands), F32),
                pltpu.SemaphoreType.REGULAR,
                dma((PUTS,)), dma((GETS,)),
                dma((ITERS,)), dma((ITERS,)),
            ],
            compiler_params=pltpu.CompilerParams(collective_id=0, has_side_effects=True),
            name="regret",
        )(*arrays)

    in_specs = (
        P("player", "leaf", None),
        P("player", "leaf", None),
        P("leaf"),
        P("player", None),
        P(),
        P("leaf", None),
        P("leaf", None),
    )
    out_specs = (P("player", "leaf", None), P("player", "leaf", None))
    return jax.shard_map(local, mesh=mesh, in_specs=in_specs, out_specs=out_specs, check_vma=False)
```

time: 33 us -> 26.7 us (0.81)
  Pallas kernels: 30.8 us -> 24.4 us
    pallas_call x1, Pallas kernels: 30.8 us -> 24.4 us  [local(): pl.pallas_call(functools.partial(kernel, n, boards, rows, hands, leaf_cou...]
where the time goes in v1:
time: 26.7 us; the launch traced here: 26.4 us
  Pallas kernels  24.4 us (91%)
  local copies, waits for them, and re-layouts  1.35 us (5%)
  between operations  0.64 us (2%)
    pallas_call x1, Pallas kernels, local(): pl.pallas_call(functools.partial(kernel, n, boards, rows, hands, leaf_cou...  24.4 us
    unnamed x2, local copies, waits for them, and re-layouts  1.35 us

profile of v1, /device:TPU:0, one launch (start us, length us, event | category | flops | bytes accessed | tf_op | source)
XLA Modules:
  0.0 26.4 jit_solution(17407347641200954827)
XLA Ops:
  0.6 24.4 %regret.1 = (f32[1,32,1326]{2,1,0:T(8,128)S(1)}, f32[1,32,1326]{2,1,0:T(8,128)S(1)}) custom-call(f32[1,32,1326]{2,1,0:T(8,128)} %refs_0_.1, f32[1,32,1326]{2,1,0:T(8,128)} %refs_1_.1, f32[1,32]{1,0:T(1,128)} %bitcast.3, s32[1,512]{1,0:T(1,128)} %refs_3_.1, s32[2,1326]{1,0:T(2,128)} %bitcast.2, s32[4,5]{1,0:T(4,128)} %refs_5_.1, s32[4,1326]{1,0:T(4,128)} %refs_6_.1), custom_call_target="tpu_custom_call" | custom-call | tf_op jit(solution)/shard_map/regret/pallas_call | solution.py:563
  25.1 0.7 %copy.11 = f32[1,32,1326]{2,1,0:T(8,128)} copy(f32[1,32,1326]{2,1,0:T(8,128)S(1)} %get-tuple-element.2) | data formatting | bytes 339456
  25.8 0.7 %copy.12 = f32[1,32,1326]{2,1,0:T(8,128)} copy(f32[1,32,1326]{2,1,0:T(8,128)S(1)} %get-tuple-element.3) | data formatting | bytes 339456

commit v2 on v1

--- a/solution.py
+++ b/solution.py
@@ -14,18 +14,18 @@
 DECK_SIZE = 52
 LANES = 128
 WIDE = 256
-SPLIT = 4
 PARTS = 2
 MESH = pl.DeviceIdType.MESH
 F32 = jnp.float32
 BF16 = jnp.bfloat16
-
-(GET_HALF, GET_BEFORE, GET_AFTER, GET_BEYOND, GET_CHANCE, GET_CHANCE_AFTER, GET_PARENT, GET_INFO,
- GET_LOW, GET_HIGH, GET_HIGHER, GET_VALUES, GET_EDGE_LOW, GET_EDGE_HIGH, GET_POLICY, GET_REGRETS, GETS) = (
-    0, 1, 3, 5, 7, 8, 10, 11, 12, 13, 14, 15, 16, 17, 18, 19, 20)
-(PUT_HALF, PUT_AFTER, PUT_BEFORE, PUT_BEYOND, PUT_CHANCE, PUT_CHANCE_BEFORE, PUT_PARENT, PUT_INFO,
- PUT_HIGH, PUT_LOW, PUT_LOWER, PUT_VALUES, PUT_EDGE, PUT_POLICY, PUT_REGRETS, PUTS) = (
-    0, 1, 2, 3, 4, 5, 6, 7, 8, 9, 10, 11, 12, 14, 15, 16)
+F8 = jnp.float8_e4m3fn
+
+(GET_HALF, GET_BEHIND, GET_NEXT, GET_AHEAD, GET_LATE, GET_AFTER, GET_BEYOND, GET_CHANCE, GET_CHANCE_AFTER, GET_PARENT,
+ GET_INFO, GET_LOW, GET_HIGH, GET_HIGHER, GET_VALUES, GET_EDGE_LOW, GET_EDGE_HIGH, GET_POLICY, GET_REGRETS, GETS) = (
+    0, 1, 3, 5, 7, 9, 11, 13, 14, 16, 17, 18, 19, 20, 21, 22, 23, 24, 25, 26)
+(PUT_HALF, PUT_BEHIND, PUT_NEXT, PUT_AHEAD, PUT_LATE, PUT_AFTER, PUT_BEYOND, PUT_CHANCE, PUT_CHANCE_BEFORE, PUT_PARENT,
+ PUT_INFO, PUT_HIGH, PUT_LOW, PUT_LOWER, PUT_VALUES, PUT_EDGE, PUT_POLICY, PUT_REGRETS, PUTS) = (
+    0, 1, 2, 3, 4, 5, 6, 7, 8, 9, 10, 11, 12, 13, 14, 15, 17, 18, 19)
 
 
 def round_up(value, unit):
@@ -56,11 +56,11 @@
 def body(
     n, boards, rows, hands, leaf_count,
     chance_far, regrets_far, pot_far, parent_far, cards_far, board_cards_far, rank_far,
-    out_regrets, out_values,
+    outs,
     chance, regrets, pot, parents, cards, board_cards, rank, load,
-    left, free, cards_wide, rank_wide, info, info_in, pots, weight,
+    codes, free, cards_wide, rank_wide, info, info_in, pots, weight,
     held, chances, policy, values, landed, standing_one, square_out, square_in,
-    last_policy, last_regrets, last_values,
+    last_policy, last_regrets, last_values, reach, behind, behind_out, ahead, ahead_out, late_before, late_after,
     all_in, put, get, square_send, square_recv,
     payoff, apart, turned, lows, right, same, same_own, same_last, split,
 ):
@@ -70,7 +70,7 @@
     spot = 2 * me + player
     hub = 2 * n - 1
     width = free.shape[1]
-    depth = left.shape[0]
+    depth = right.shape[0]
     half = boards // 2
     near = half + 1
     local = boards * rows
@@ -104,6 +104,10 @@
         chances[p, own:] = jnp.zeros((rows, hands), F32)
         values[0, p, :rows] = jnp.zeros((rows, hands), F32)
         landed[p] = jnp.zeros((2 * rows, hands), F32)
+        behind[p] = jnp.zeros((1, hands), F32)
+        ahead[p] = jnp.zeros((rows, hands), F32)
+        late_before[p] = jnp.zeros((rows, hands), F32)
+        late_after[p] = jnp.zeros((2 * rows, hands), F32)
     last_values[:rows] = jnp.zeros((rows, hands), F32)
     last_values[rows + local :] = jnp.zeros((rows, hands), F32)
 
@@ -148,15 +152,13 @@
     touched = jnp.dot(on_board.astype(BF16), holding.astype(BF16), preferred_element_type=F32)
     untouched = (touched < 0.5).astype(F32)
     first = player == 0
-    left[...] = holding + valid
-    left[DECK_SIZE : DECK_SIZE + half, :] = jnp.where(first, code[:half], code[half:boards])
-    left[DECK_SIZE + half : DECK_SIZE + near, :] = code[half : half + 1]
+    turned[...] = (holding + valid).T.astype(F8)
+    codes[...] = jnp.zeros(codes.shape, F32)
+    codes[:half] = jnp.where(first, code[:half], code[half:boards])
+    codes[half:near] = code[half : half + 1]
     free[:half] = jnp.where(first, untouched[:half], untouched[half:])
     free[half:near] = untouched[half : half + 1]
-    right[:, :width] = (valid - holding).astype(BF16)
-    pick = lax.broadcasted_iota(jnp.int32, (depth, near * LANES), 0) - DECK_SIZE
-    at_lane = lax.broadcasted_iota(jnp.int32, (depth, near * LANES), 1)
-    right[:, width:] = ((at_lane >= pick * LANES) & (at_lane < pick * LANES + LANES)).astype(BF16)
+    right[...] = (valid - holding).astype(F8)
     info[...] = jnp.zeros(info.shape, F32)
     info[:, :width] = code[:1]
     info[:, width : 2 * width] = untouched[:1]
@@ -168,8 +170,6 @@
         (span, LANES))
     split[...] = jnp.zeros(split.shape, BF16)
 
-    turned[...] = left[...].T.astype(BF16)
-
     blocks = width // LANES
     length = width // PARTS
 
@@ -181,40 +181,53 @@
                 apart[c + k] = found[:, k * LANES : (k + 1) * LANES].reshape(PARTS, length, LANES)
 
     def lower(begin, count):
-        found = jnp.dot(
-            turned[...], right[:, width + begin * LANES : width + (begin + count) * LANES],
-            preferred_element_type=F32).astype(BF16)
+        columns = codes[...].T
         for b in range(count):
-            lows[b] = found[:, b * LANES : (b + 1) * LANES].reshape(PARTS, length, LANES)
+            lows[b] = jnp.broadcast_to(
+                columns[:, begin + b : begin + b + 1], (width, LANES)).astype(BF16).reshape(PARTS, length, LANES)
 
     def build(begin, count):
         def column(c, carry):
             at = pl.multiple_of(c * LANES, LANES)
             highs = [
                 jnp.broadcast_to(
-                    left[DECK_SIZE + begin + b : DECK_SIZE + begin + b + 1, pl.ds(at, LANES)], (16, LANES)).astype(BF16)
+                    codes[begin + b : begin + b + 1, pl.ds(at, LANES)], (32, LANES)).astype(BF16)
                 for b in range(count)]
 
             def part(k, carry):
-                for r in range(0, length, 16):
-                    bound = apart[c, k, r : r + 16]
+                for r in range(0, length, 32):
+                    bound = apart[c, k, r : r + 32]
                     floor = -bound
                     for b in range(count):
-                        gap = highs[b] - lows[b, k, r : r + 16]
-                        payoff[begin + b, c, k, r : r + 16] = jnp.minimum(jnp.maximum(gap, floor), bound)
+                        gap = highs[b] - lows[b, k, r : r + 32]
+                        payoff[begin + b, c, k, r : r + 32] = jnp.minimum(jnp.maximum(gap, floor), bound).astype(F8)
                 return carry
 
             return lax.fori_loop(0, PARTS, part, carry)
 
         return column
-
-    separate(0, blocks)
-    lower(0, half)
-    lax.fori_loop(0, SPLIT, build(0, half), 0)
 
     for copy in loads[4:]:
         copy.wait()
 
+    def ids_of(p, begin, count):
+        leaf = begin + lax.broadcasted_iota(jnp.int32, (count, leaf_count), 0)
+        here = lax.broadcasted_iota(jnp.int32, (count, leaf_count), 1)
+        return jnp.sum(jnp.where(leaf == here, parents[p].astype(F32) + 1.0, 0.0), axis=1, keepdims=True)
+
+    found = ids_of(player, me * local - rows, 3 * rows)
+    positive = jnp.maximum(regrets[0, : 2 * rows], 0.0) + DELTA
+    shared = (found[rows : 2 * rows] == found[rows - 1 : rows]) & (found[rows - 1 : rows] > 0.0)
+    partial = node_totals(same_of(found[rows:]), positive)[:rows]
+    ahead_out[...] = chance[0, :rows] * positive[:rows] / jnp.where(shared, 1.0, partial)
+    found = ids_of(player, (me + 1) * local - rows, rows)
+    positive = jnp.maximum(regrets[0, local - rows :], 0.0) + DELTA
+    behind_out[...] = jnp.sum(jnp.where(found == found[rows - 1 :], positive, 0.0), axis=0, keepdims=True)
+
+    @pl.when(me == 0)
+    def _():
+        separate(0, blocks)
+
     @pl.when(spot < hub)
     def _():
         pl.semaphore_wait(barrier, 1 + (me > 0).astype(jnp.int32) + (me < n - 1).astype(jnp.int32))
@@ -223,12 +236,9 @@
     def _():
         pl.semaphore_wait(barrier, 2 * n - 1)
 
-        def welcome(k, carry):
-            pl.semaphore_signal(
-                all_in, inc=1, device_id=device_at(lax.rem(spot + k, 2 * n)), device_id_type=MESH)
-            return carry
-
-        lax.fori_loop(1, 2 * n, welcome, 0)
+    @pl.when(me < n - 1)
+    def _():
+        push(behind_out, behind.at[player], {"leaf": me + 1, "player": 0}, PUT_BEHIND, GET_BEHIND + player)
 
     @pl.when(me > 0)
     def _():
@@ -238,17 +248,8 @@
         def _():
             push(info, info_in, to, PUT_INFO, GET_INFO)
 
-        push(regrets.at[0, pl.ds(0, rows)], held.at[player, pl.ds(rows + own, rows)], to, PUT_BEFORE, GET_AFTER + player)
-        push(
-            regrets.at[0, pl.ds(rows, rest)], held.at[player, pl.ds(2 * rows + own, rest)], to, PUT_BEYOND,
-            GET_BEYOND + player)
-        push(chance.at[0, pl.ds(0, edge)], chances.at[player, pl.ds(own, edge)], to, PUT_CHANCE_BEFORE, GET_CHANCE_AFTER + player)
-
-    @pl.when(me < n - 1)
-    def _():
-        push(
-            regrets.at[0, pl.ds(local - edge, edge)], held.at[player, pl.ds(rows - edge, edge)],
-            {"leaf": me + 1, "player": 0}, PUT_AFTER, GET_BEFORE + player)
+        push(regrets.at[0, pl.ds(0, edge)], held.at[player, pl.ds(rows + own, edge)], to, PUT_NEXT, GET_NEXT + player)
+        push(ahead_out.at[pl.ds(0, edge)], ahead.at[player, pl.ds(0, edge)], to, PUT_AHEAD, GET_AHEAD + player)
 
     push(parents.at[player], parents.at[player], partner, PUT_PARENT, GET_PARENT)
 
@@ -266,14 +267,39 @@
         held[1, : own + rows] = regrets[0, own - rows :]
         chances[1, :own] = chance[0, own:]
 
-    lax.fori_loop(SPLIT, blocks, build(0, half), 0)
+    @pl.when(spot == hub)
+    def _():
+        def welcome(k, carry):
+            pl.semaphore_signal(
+                all_in, inc=1, device_id=k - 1, device_id_type=pl.DeviceIdType.LOGICAL)
+            return carry
+
+        lax.fori_loop(1, 2 * n, welcome, 0)
+
+    @pl.when(me > 0)
+    def _():
+        separate(0, blocks)
+
+    lower(0, half)
+    lax.fori_loop(0, blocks, build(0, half), 0)
+
+    @pl.when(me < n - 1)
+    def _():
+        push(
+            regrets.at[0, pl.ds(local - edge, edge)], late_before.at[player, pl.ds(rows - edge, edge)],
+            {"leaf": me + 1, "player": 0}, PUT_LATE, GET_LATE + player)
+
+    @pl.when(me > 0)
+    def _():
+        to = {"leaf": me - 1, "player": 1}
+        push(
+            regrets.at[0, pl.ds(edge, rows - edge)], late_after.at[player, pl.ds(edge, rows - edge)], to, PUT_AFTER,
+            GET_AFTER + player)
+        push(
+            regrets.at[0, pl.ds(rows, rest)], late_after.at[player, pl.ds(rows, rest)], to, PUT_BEYOND,
+            GET_BEYOND + player)
 
     settle(parents.at[other], get.at[GET_PARENT])
-
-    def ids_of(p, begin, count):
-        leaf = begin + lax.broadcasted_iota(jnp.int32, (count, leaf_count), 0)
-        here = lax.broadcasted_iota(jnp.int32, (count, leaf_count), 1)
-        return jnp.sum(jnp.where(leaf == here, parents[p].astype(F32) + 1.0, 0.0), axis=1, keepdims=True)
 
     ids = []
     weights = []
@@ -294,7 +320,7 @@
     @pl.when((player == 1) & (me < n - 1))
     def _():
         settle(info_in, get.at[GET_INFO])
-        left[DECK_SIZE + half : DECK_SIZE + near, :] = info_in[:, :width]
+        codes[half:near] = info_in[:, :width]
         free[half:near] = info_in[:, width : 2 * width]
         pots[own:] = jnp.broadcast_to(
             jnp.sum(
@@ -302,21 +328,19 @@
                 axis=1, keepdims=True),
             (rows, LANES))
 
-    turned[...] = left[...].T.astype(BF16)
     lower(half, 1)
     lax.fori_loop(0, blocks, build(half, 1), 0)
 
     @pl.when((player == 0) & (me > 0))
     def _():
         for p in range(2):
-            settle(held.at[p, pl.ds(rows - edge, edge)], get.at[GET_BEFORE + p])
+            settle(behind.at[p], get.at[GET_BEHIND + p])
 
     @pl.when((player == 1) & (me < n - 1))
     def _():
         for p in range(2):
-            settle(held.at[p, pl.ds(rows + own, rows)], get.at[GET_AFTER + p])
-            settle(held.at[p, pl.ds(2 * rows + own, rest)], get.at[GET_BEYOND + p])
-            settle(chances.at[p, pl.ds(own, edge)], get.at[GET_CHANCE_AFTER + p])
+            settle(held.at[p, pl.ds(rows + own, edge)], get.at[GET_NEXT + p])
+            settle(ahead.at[p, pl.ds(0, edge)], get.at[GET_AHEAD + p])
 
     @pl.when(player == 0)
     def _():
@@ -328,10 +352,34 @@
         settle(held.at[0, pl.ds(0, own + rows)], get.at[GET_HALF])
         settle(chances.at[0, pl.ds(0, own)], get.at[GET_CHANCE])
 
-    standing = held[...].reshape(2 * total, hands)
+    def strategy(standing):
+        positive = jnp.maximum(standing, 0.0) + DELTA
+        return positive / node_totals(same[...], positive)
+
     for it in range(ITERS):
-        positive = jnp.maximum(standing, 0.0) + DELTA
-        policy[it] = (positive / node_totals(same[...], positive)).reshape(2, total, hands)
+        if it == 0:
+            at = lax.broadcasted_iota(jnp.int32, (2 * total, 1), 0)
+            at = jnp.where(at >= total, at - total, at)
+            present = ((player == 0) & (at >= rows)) | ((player == 1) & (at < rows + own + edge))
+            positive = jnp.where(present, jnp.maximum(held[...].reshape(2 * total, hands), 0.0) + DELTA, 0.0)
+            totals = node_totals(same[...], positive)
+            for p in range(2):
+                found = ids[p]
+                mine = slice(p * total + rows, p * total + rows + own)
+                beside = slice(mine.stop, mine.stop + rows)
+                back = (found[rows : rows + own] == found[rows - 1 : rows]) & (found[rows - 1 : rows] > 0.0)
+                forth = found[rows + own : rows + span] == found[rows + own - 1 : rows + own]
+                choice = positive[mine] / (totals[mine] + jnp.where(back, behind[p], 0.0))
+                policy[0, p, rows : rows + own] = choice
+                reach[p, :own] = chances[p, :own] * choice
+                policy[0, p, rows + own : rows + span] = positive[beside] / jnp.where(forth, totals[beside], 1.0)
+                reach[p, own:] = jnp.where(player == 0, chances[p, own:] * positive[beside], ahead[p]) / jnp.where(
+                    forth | (player == 0), totals[beside], 1.0)
+        else:
+            policy[it] = strategy(standing).reshape(2, total, hands)
+            for p in range(2):
+                reach[p, :own] = chances[p, :own] * policy[it, p, rows : rows + own]
+                reach[p, own:] = chances[p, own:] * policy[it, p, rows + own : rows + span]
         if it == last:
             standing_one[...] = standing.reshape(2, total, hands)
             push(
@@ -345,7 +393,7 @@
             seen = slice(b * rows, (b + 1) * rows)
             kept = slice((b + 1) * rows, (b + 2) * rows)
             open_hands = free[b : b + 1, :]
-            facing = jnp.concatenate([chances[p, seen] * policy[it, p, kept] for p in range(2)], axis=0)
+            facing = jnp.concatenate([reach[p, seen] for p in range(2)], axis=0)
             facing = facing * open_hands[:, :hands]
             coarse = facing.astype(BF16).astype(F32)
             split[b, :, :hands] = jnp.concatenate([coarse, facing - coarse], axis=0).astype(BF16)
@@ -405,14 +453,39 @@
             def _():
                 pl.semaphore_wait(all_in, 1)
 
-        def tell(k, carry, it=it):
+        def tell(t, carry, it=it):
+            at = t if it == last else jnp.where(spot < n, 2 * n - 2 - t, t)
+            ahead = (at >= spot).astype(jnp.int32)
             pltpu.make_async_remote_copy(
-                src_ref=square_out.at[it], dst_ref=square_in.at[it, k - 1],
+                src_ref=square_out.at[it], dst_ref=square_in.at[it, spot - 1 + ahead],
                 send_sem=square_send.at[it], recv_sem=square_recv.at[it],
-                device_id=device_at(lax.rem(spot + k, 2 * n)), device_id_type=MESH).start()
+                device_id=at + ahead, device_id_type=pl.DeviceIdType.LOGICAL).start()
             return carry
 
-        lax.fori_loop(1, 2 * n, tell, 0)
+        lax.fori_loop(0, 2 * n - 1, tell, 0)
+
+        if it == 0:
+            @pl.when((player == 0) & (me > 0))
+            def _():
+                for p in range(2):
+                    settle(late_before.at[p, pl.ds(rows - edge, edge)], get.at[GET_LATE + p])
+
+            @pl.when((player == 1) & (me < n - 1))
+            def _():
+                for p in range(2):
+                    settle(late_after.at[p, pl.ds(edge, rows - edge)], get.at[GET_AFTER + p])
+                    settle(late_after.at[p, pl.ds(rows, rest)], get.at[GET_BEYOND + p])
+
+            standing = jnp.concatenate([
+                part for p in range(2) for part in (
+                    held[p, :rows] + late_before[p], held[p, rows : rows + own],
+                    held[p, rows + own :] + late_after[p])], axis=0)
+            policy[0] = strategy(standing).reshape(2, total, hands)
+            for p in range(2):
+                beside = slice(p * total + rows + own, p * total + rows + span)
+                forth = ids[p][rows + own : rows + span] == ids[p][rows + own - 1 : rows + own]
+                factor = jnp.where(forth, jnp.maximum(standing[beside], 0.0) + DELTA, policy[0, p, rows + own : rows + span])
+                chances[p, own:] = jnp.where(player == 0, chances[p, own:], ahead[p] / factor)
 
         if it < last:
             @pl.when(spot > 0)
@@ -449,7 +522,7 @@
 
             gained = last_values[...]
             instant = (gained - node_totals(same_last[...], last_policy[...] * gained))[rows : rows + local]
-            out_values[0] = gained[rows : rows + local]
+            outs[1] = gained[rows : rows + local]
 
         everyone = square_in.at[it]
         settle(everyone, square_recv.at[it])
@@ -460,7 +533,7 @@
             turn = lax.broadcasted_iota(jnp.int32, (2 * total, 1), 0) < total
             standing = standing + instant * jnp.where(turn, inverse[0:1, :1], inverse[1:2, :1])
         else:
-            out_regrets[0] = last_regrets[...] + instant * jnp.where(player == 0, inverse[0:1, :1], inverse[1:2, :1])
+            outs[0] = last_regrets[...] + instant * jnp.where(player == 0, inverse[0:1, :1], inverse[1:2, :1])
 
     def sent(view, slot):
         settle(view, put.at[slot])
@@ -471,13 +544,15 @@
         def _():
             sent(info, PUT_INFO)
 
-        sent(regrets.at[0, pl.ds(0, rows)], PUT_BEFORE)
+        sent(regrets.at[0, pl.ds(0, edge)], PUT_NEXT)
+        sent(ahead_out.at[pl.ds(0, edge)], PUT_AHEAD)
+        sent(regrets.at[0, pl.ds(edge, rows - edge)], PUT_AFTER)
         sent(regrets.at[0, pl.ds(rows, rest)], PUT_BEYOND)
-        sent(chance.at[0, pl.ds(0, edge)], PUT_CHANCE_BEFORE)
 
     @pl.when(me < n - 1)
     def _():
-        sent(regrets.at[0, pl.ds(local - edge, edge)], PUT_AFTER)
+        sent(behind_out, PUT_BEHIND)
+        sent(regrets.at[0, pl.ds(local - edge, edge)], PUT_LATE)
 
     sent(parents.at[player], PUT_PARENT)
 
@@ -526,14 +601,14 @@
     total = span + 2 * rows
     edged = (boards + 2) * rows
     width = round_up(hands, LANES)
-    depth = round_up(DECK_SIZE + near + 1, 16)
+    depth = round_up(DECK_SIZE + 1, 32)
     pl.run_scoped(
         functools.partial(body, n, boards, rows, hands, leaf_count, *refs),
-        pltpu.VMEM((near, width // LANES, PARTS, width // PARTS, LANES), BF16),
+        pltpu.VMEM((near, width // LANES, PARTS, width // PARTS, LANES), F8),
         pltpu.VMEM((width // LANES, PARTS, width // PARTS, LANES), BF16),
-        pltpu.VMEM((width, depth), BF16),
+        pltpu.VMEM((width, depth), F8),
         pltpu.VMEM((near, PARTS, width // PARTS, LANES), BF16),
-        pltpu.VMEM((depth, width + near * LANES), BF16),
+        pltpu.VMEM((depth, width), F8),
         pltpu.VMEM((2 * total, 4 * total), BF16),
         pltpu.VMEM((2 * span, 4 * span), BF16),
         pltpu.VMEM((edged, 2 * edged), BF16),
@@ -552,7 +627,6 @@
         width = round_up(hands, LANES)
         half = boards // 2
         near = half + 1
-        depth = round_up(DECK_SIZE + near + 1, 16)
         span = near * rows
         total = (half + 3) * rows
         edged = leaf_rows + 2 * rows
@@ -560,11 +634,11 @@
         shape = pltpu.VMEM(chance_reach.shape, F32)
         dma = pltpu.SemaphoreType.DMA
         arrays = (chance_reach, regrets_start, pot[None], parent, hand_cards.T, board_cards, hand_rank)
-        return pl.pallas_call(
+        outs = pl.pallas_call(
             functools.partial(kernel, n, boards, rows, hands, leaf_count),
-            out_shape=(shape, shape),
+            out_shape=pltpu.VMEM((2, leaf_rows, hands), F32),
             in_specs=[pl.BlockSpec(memory_space=pl.ANY)] * len(arrays),
-            out_specs=(vmem, vmem),
+            out_specs=vmem,
             scratch_shapes=[
                 pltpu.VMEM(chance_reach.shape, F32),
                 pltpu.VMEM(regrets_start.shape, F32),
@@ -574,7 +648,7 @@
                 pltpu.VMEM(board_cards.shape, jnp.int32),
                 pltpu.VMEM(hand_rank.shape, jnp.int32),
                 dma((len(arrays),)),
-                pltpu.VMEM((depth, width), F32),
+                pltpu.VMEM((round_up(near, 8), width), F32),
                 pltpu.VMEM((near, width), F32),
                 pltpu.VMEM((2, width), jnp.int32),
                 pltpu.VMEM((round_up(boards, 8), width), jnp.int32),
@@ -593,6 +667,13 @@
                 pltpu.VMEM((edged, hands), F32),
                 pltpu.VMEM((leaf_rows, hands), F32),
                 pltpu.VMEM((edged, hands), F32),
+                pltpu.VMEM((2, span, hands), F32),
+                pltpu.VMEM((2, 1, hands), F32),
+                pltpu.VMEM((1, hands), F32),
+                pltpu.VMEM((2, rows, hands), F32),
+                pltpu.VMEM((rows, hands), F32),
+                pltpu.VMEM((2, rows, hands), F32),
+                pltpu.VMEM((2, 2 * rows, hands), F32),
                 pltpu.SemaphoreType.REGULAR,
                 dma((PUTS,)), dma((GETS,)),
                 dma((ITERS,)), dma((ITERS,)),
@@ -600,6 +681,7 @@
             compiler_params=pltpu.CompilerParams(collective_id=0, has_side_effects=True),
             name="regret",
         )(*arrays)
+        return outs[:1], outs[1:]
 
     in_specs = (
         P("player", "leaf", None),

time: 26.7 us -> 22.2 us (0.83)
  Pallas kernels: 24.4 us -> 20.6 us
  local copies, waits for them, and re-layouts: 1.35 us -> 0.76 us
    pallas_call x1, Pallas kernels: 24.4 us -> 20.6 us  [local(): pl.pallas_call(functools.partial(kernel, n, boards, rows, hands, leaf_cou...]
    unnamed x2 -> x0, local copies, waits for them, and re-layouts: 1.35 us -> none
    slice x0 -> x1, local copies, waits for them, and re-layouts: none -> 0.76 us  [local(): return (outs[:1], outs[1:])]
where the time goes in v2:
time: 22.2 us; the launch traced here: 21.9 us
  Pallas kernels  20.6 us (93%)
  local copies, waits for them, and re-layouts  0.76 us (3%)
  between operations  0.64 us (3%)
    pallas_call x1, Pallas kernels, local(): pl.pallas_call(functools.partial(kernel, n, boards, rows, hands, leaf_cou...  20.6 us
    slice x1, local copies, waits for them, and re-layouts, local(): return (outs[:1], outs[1:])  0.76 us

profile of v2, /device:TPU:0, one launch (start us, length us, event | category | flops | bytes accessed | tf_op | source)
XLA Modules:
  0.0 21.9 jit_solution(9334225691255636104)
XLA Ops:
  0.6 20.6 %regret.1 = f32[2,32,1326]{2,1,0:T(8,128)S(1)} custom-call(f32[1,32,1326]{2,1,0:T(8,128)} %refs_0_.1, f32[1,32,1326]{2,1,0:T(8,128)} %refs_1_.1, f32[1,32]{1,0:T(1,128)} %bitcast.3, s32[1,512]{1,0:T(1,128)} %refs_3_.1, s32[2,1326]{1,0:T(2,128)} %bitcast.2, s32[4,5]{1,0:T(4,128)} %refs_5_.1, s32[4,1326]{1,0:T(4,128)} %refs_6_.1), custom_call_target="tpu_custom_call" | custom-call | tf_op jit(solution)/shard_map/regret/pallas_call | solution.py:637
  21.2 0.8 %fusion = (f32[1,32,1326]{2,1,0:T(8,128)}, f32[1,32,1326]{2,1,0:T(8,128)}) fusion(f32[2,32,1326]{2,1,0:T(8,128)S(1)} %regret.1), kind=kLoop, calls=%fused_computation | loop fusion | bytes 678912 | tf_op jit(solution)/shard_map/slice | solution.py:684

commit v3 on v2

--- a/solution.py
+++ b/solution.py
@@ -14,7 +14,7 @@
 DECK_SIZE = 52
 LANES = 128
 WIDE = 256
-PARTS = 2
+PARTS = 1
 MESH = pl.DeviceIdType.MESH
 F32 = jnp.float32
 BF16 = jnp.bfloat16
@@ -236,6 +236,10 @@
     def _():
         pl.semaphore_wait(barrier, 2 * n - 1)
 
+    @pl.when((player == 1) & (me > 0))
+    def _():
+        push(info, info_in, {"leaf": me - 1, "player": 1}, PUT_INFO, GET_INFO)
+
     @pl.when(me < n - 1)
     def _():
         push(behind_out, behind.at[player], {"leaf": me + 1, "player": 0}, PUT_BEHIND, GET_BEHIND + player)
@@ -243,11 +247,6 @@
     @pl.when(me > 0)
     def _():
         to = {"leaf": me - 1, "player": 1}
-
-        @pl.when(player == 1)
-        def _():
-            push(info, info_in, to, PUT_INFO, GET_INFO)
-
         push(regrets.at[0, pl.ds(0, edge)], held.at[player, pl.ds(rows + own, edge)], to, PUT_NEXT, GET_NEXT + player)
         push(ahead_out.at[pl.ds(0, edge)], ahead.at[player, pl.ds(0, edge)], to, PUT_AHEAD, GET_AHEAD + player)
 
@@ -314,7 +313,6 @@
         weights.append(counted.astype(F32))
     same[...] = same_of(jnp.concatenate(ids, axis=0))
     same_own[...] = same_of(jnp.concatenate([found[rows : rows + span] for found in ids], axis=0))
-    same_last[...] = same_of(ids_of(player, me * local - rows, local + 2 * rows))
     weight[...] = jnp.broadcast_to(jnp.concatenate(weights, axis=0), (2 * span, LANES))
 
     @pl.when((player == 1) & (me < n - 1))
@@ -408,6 +406,13 @@
             summed = summed * open_hands[:, :hands] * stake
             values[it, 1, kept] = summed[:rows]
             values[it, 0, kept] = summed[rows:]
+            if b == 0 and it < last:
+                @pl.when(spot > 0)
+                def _(it=it):
+                    push(
+                        values.at[it, :, pl.ds(rows + edge, rows - edge)], landed.at[:, pl.ds(edge, rows - edge)],
+                        device_at(spot - 1), PUT_LOW, GET_HIGH)
+
             if b == half - 1 and it < last:
                 @pl.when(spot < hub)
                 def _(it=it):
@@ -417,9 +422,6 @@
 
                 @pl.when(spot > 0)
                 def _(it=it):
-                    push(
-                        values.at[it, :, pl.ds(rows + edge, rows - edge)], landed.at[:, pl.ds(edge, rows - edge)],
-                        device_at(spot - 1), PUT_LOW, GET_HIGH)
                     push(
                         values.at[it, :, pl.ds(2 * rows, rest)], landed.at[:, pl.ds(rows, rest)],
                         device_at(spot - 1), PUT_LOWER, GET_HIGHER)
@@ -465,6 +467,7 @@
         lax.fori_loop(0, 2 * n - 1, tell, 0)
 
         if it == 0:
+            same_last[...] = same_of(ids_of(player, me * local - rows, local + 2 * rows))
             @pl.when((player == 0) & (me > 0))
             def _():
                 for p in range(2):

time: 22.2 us -> 22.1 us (level)
  no operation moved by 1% of the time
where the time goes in v3:
time: 22.1 us; the launch traced here: 21.8 us
  Pallas kernels  20.5 us (93%)
  local copies, waits for them, and re-layouts  0.76 us (3%)
  between operations  0.64 us (3%)
    pallas_call x1, Pallas kernels, local(): pl.pallas_call(functools.partial(kernel, n, boards, rows, hands, leaf_cou...  20.5 us
    slice x1, local copies, waits for them, and re-layouts, local(): return (outs[:1], outs[1:])  0.76 us

profile of v3, /device:TPU:0, one launch (start us, length us, event | category | flops | bytes accessed | tf_op | source)
XLA Modules:
  0.0 21.8 jit_solution(11098122831146952528)
XLA Ops:
  0.6 20.5 %regret.1 = f32[2,32,1326]{2,1,0:T(8,128)S(1)} custom-call(f32[1,32,1326]{2,1,0:T(8,128)} %refs_0_.1, f32[1,32,1326]{2,1,0:T(8,128)} %refs_1_.1, f32[1,32]{1,0:T(1,128)} %bitcast.3, s32[1,512]{1,0:T(1,128)} %refs_3_.1, s32[2,1326]{1,0:T(2,128)} %bitcast.2, s32[4,5]{1,0:T(4,128)} %refs_5_.1, s32[4,1326]{1,0:T(4,128)} %refs_6_.1), custom_call_target="tpu_custom_call" | custom-call | tf_op jit(solution)/shard_map/regret/pallas_call | solution.py:640
  21.1 0.8 %fusion = (f32[1,32,1326]{2,1,0:T(8,128)}, f32[1,32,1326]{2,1,0:T(8,128)}) fusion(f32[2,32,1326]{2,1,0:T(8,128)S(1)} %regret.1), kind=kLoop, calls=%fused_computation | loop fusion | bytes 678912 | tf_op jit(solution)/shard_map/slice | solution.py:687

commit v4 on v3

--- a/solution.py
+++ b/solution.py
@@ -378,15 +378,6 @@
             for p in range(2):
                 reach[p, :own] = chances[p, :own] * policy[it, p, rows : rows + own]
                 reach[p, own:] = chances[p, own:] * policy[it, p, rows + own : rows + span]
-        if it == last:
-            standing_one[...] = standing.reshape(2, total, hands)
-            push(
-                policy.at[it, other, pl.ds(pl.multiple_of(player * rows, rows), span)],
-                last_policy.at[pl.ds(pl.multiple_of(player * span, rows), span)], partner, PUT_POLICY, GET_POLICY)
-            push(
-                standing_one.at[other, pl.ds(rows, own)], last_regrets.at[pl.ds(pl.multiple_of(player * own, rows), own)],
-                partner, PUT_REGRETS, GET_REGRETS)
-
         for b in range(near):
             seen = slice(b * rows, (b + 1) * rows)
             kept = slice((b + 1) * rows, (b + 2) * rows)
@@ -465,6 +456,15 @@
             return carry
 
         lax.fori_loop(0, 2 * n - 1, tell, 0)
+
+        if it == last:
+            standing_one[...] = standing.reshape(2, total, hands)
+            push(
+                policy.at[it, other, pl.ds(pl.multiple_of(player * rows, rows), span)],
+                last_policy.at[pl.ds(pl.multiple_of(player * span, rows), span)], partner, PUT_POLICY, GET_POLICY)
+            push(
+                standing_one.at[other, pl.ds(rows, own)], last_regrets.at[pl.ds(pl.multiple_of(player * own, rows), own)],
+                partner, PUT_REGRETS, GET_REGRETS)
 
         if it == 0:
             same_last[...] = same_of(ids_of(player, me * local - rows, local + 2 * rows))

time: 22.1 us -> 22 us (level)
  no operation moved by 1% of the time
where the time goes in v4:
time: 22 us; the launch traced here: 21.8 us
  Pallas kernels  20.4 us (93%)
  local copies, waits for them, and re-layouts  0.76 us (3%)
  between operations  0.64 us (3%)
    pallas_call x1, Pallas kernels, local(): pl.pallas_call(functools.partial(kernel, n, boards, rows, hands, leaf_cou...  20.4 us
    slice x1, local copies, waits for them, and re-layouts, local(): return (outs[:1], outs[1:])  0.76 us

profile of v4, /device:TPU:0, one launch (start us, length us, event | category | flops | bytes accessed | tf_op | source)
XLA Modules:
  0.0 21.8 jit_solution(13307804597363858821)
XLA Ops:
  0.6 20.4 %regret.1 = f32[2,32,1326]{2,1,0:T(8,128)S(1)} custom-call(f32[1,32,1326]{2,1,0:T(8,128)} %refs_0_.1, f32[1,32,1326]{2,1,0:T(8,128)} %refs_1_.1, f32[1,32]{1,0:T(1,128)} %bitcast.3, s32[1,512]{1,0:T(1,128)} %refs_3_.1, s32[2,1326]{1,0:T(2,128)} %bitcast.2, s32[4,5]{1,0:T(4,128)} %refs_5_.1, s32[4,1326]{1,0:T(4,128)} %refs_6_.1), custom_call_target="tpu_custom_call" | custom-call | tf_op jit(solution)/shard_map/regret/pallas_call | solution.py:640
  21.0 0.8 %fusion = (f32[1,32,1326]{2,1,0:T(8,128)}, f32[1,32,1326]{2,1,0:T(8,128)}) fusion(f32[2,32,1326]{2,1,0:T(8,128)S(1)} %regret.1), kind=kLoop, calls=%fused_computation | loop fusion | bytes 678912 | tf_op jit(solution)/shard_map/slice | solution.py:687
